TPU v7x, 32 devices: a whole 2x2x4 slice. The times are simulated.
32 devices in a mesh: rows: 8 (over z, x), grp: 4 (over y, core).
Axes of the slice: x: 2, y: 2, z: 4, core: 2. Of those that a mesh axis runs over, the one named last changes fastest.
Arguments:
- queries: bfloat16 [2048, 1024], P('rows'), may hold values from -12 to 12
- passages: bfloat16 [8192, 1024], P(('rows', 'grp')), may hold values from -12 to 12
- positive: int32 [2048], P('rows'), may hold values from 0 to 8191
Outputs:
- losses: float32 [2048], P('rows')
- grad_queries: float32 [2048, 1024], P('rows')
- grad_passages: float32 [8192, 1024], P(('rows', 'grp'))
All inputs are finite; a program needn't handle non-finite values.
Results may differ from a plain program's by a relative error of at most 0.0015.
Values may be sent and summed in bfloat16 or wider, within the bound.
A program may use at most 128 MiB of HBM per device.

v0:
```python
import math
import jax
import jax.numpy as jnp
from jax import lax
from jax.sharding import PartitionSpec as P

lowest = -1e30


def combined_all(value, axis, combine):
    everything = jax.tree.map(lambda part: lax.all_gather(part, axis), value)
    leading = jax.tree.map(lambda part: part[0], everything)

    def step(k, so_far):
        return combine(so_far, jax.tree.map(lambda part: part[k], everything))

    return lax.fori_loop(1, lax.axis_size(axis), step, leading)


def score_block(left_rows, right_rows):
    return lax.dot_general(
        left_rows, right_rows, (((1,), (1,)), ((), ())), preferred_element_type=jnp.float32
    )


def block_size(length):
    return math.gcd(length, 1024)


def combine_parts(first_part, second_part):
    left_max, left_sum, left_pos = first_part
    right_max, right_sum, right_pos = second_part
    joined = jnp.maximum(left_max, right_max)
    merged_sum = left_sum * jnp.exp(left_max - joined) + right_sum * jnp.exp(right_max - joined)
    return (joined, merged_sum, left_pos + right_pos)


def local(queries, passages, positive):
    per_dev = passages.shape[0]
    rows_q = queries.shape[0]
    width = queries.shape[1]
    groups = lax.axis_size("grp")
    group_id = lax.axis_index("grp")
    row_id = lax.axis_index("rows")
    block_id = positive // per_dev
    local_row = positive % per_dev
    share_pos = jnp.where(
        block_id % groups == group_id, block_id // groups * per_dev + local_row, -1
    )
    initial = (
        jnp.full((rows_q,), lowest, jnp.float32),
        jnp.zeros((rows_q,), jnp.float32),
        jnp.zeros((rows_q,), jnp.float32),
    )
    segment = lax.all_gather(passages, "rows", axis=0, tiled=True)
    length = segment.shape[0]
    block_rows = block_size(length)

    def forward_inner_step(block_index, state):
        running_max, running_sum, chosen = state
        first = block_index * block_rows
        sub_block = lax.dynamic_slice_in_dim(segment, first, block_rows, 0)
        scores = score_block(queries, sub_block)
        column = first + lax.iota(jnp.int32, block_rows)
        chosen = chosen + jnp.sum(
            jnp.where(share_pos[:, None] == column[None, :], scores, 0.0), axis=1
        )
        newbest = jnp.maximum(running_max, jnp.max(scores, axis=1))
        running_sum = running_sum * jnp.exp(running_max - newbest) + jnp.sum(
            jnp.exp(scores - newbest[:, None]), axis=1
        )
        return (newbest, running_sum, chosen)

    partial_state = lax.fori_loop(0, length // block_rows, forward_inner_step, initial)
    running_max, running_sum, chosen = combined_all(partial_state, "grp", combine_parts)
    log_total = running_max + jnp.log(running_sum)
    losses = log_total - chosen
    all_lse, all_positive = (
        lax.all_gather(log_total, "rows", axis=0, tiled=True),
        lax.all_gather(positive, "rows", axis=0, tiled=True),
    )
    own_base = (row_id * groups + group_id) * per_dev
    query_start = jnp.zeros((rows_q, width), jnp.float32)
    passage_start = jnp.zeros((per_dev, width), jnp.float32)
    query_segment = lax.all_gather(passages, "rows", axis=0, tiled=True)
    length = query_segment.shape[0]
    query_block_rows = block_size(length)

    def query_inner_step(block_index, accum):
        first = block_index * query_block_rows
        sub_block = lax.dynamic_slice_in_dim(query_segment, first, query_block_rows, 0)
        scores = score_block(queries, sub_block)
        weights = jnp.exp(scores - log_total[:, None]).astype(jnp.bfloat16)
        accum = accum + jnp.dot(weights, sub_block, preferred_element_type=jnp.float32)
        hit_row = share_pos - first
        inside = (hit_row >= 0) & (hit_row < query_block_rows)
        picked = jnp.take(sub_block, jnp.clip(hit_row, 0, query_block_rows - 1), axis=0).astype(
            jnp.float32
        )
        return accum - jnp.where(inside[:, None], picked, 0.0)

    query_part = lax.fori_loop(0, length // query_block_rows, query_inner_step, query_start)
    passage_segment = lax.all_gather(queries, "rows", axis=0, tiled=True)
    length = passage_segment.shape[0]
    passage_block_rows = block_size(length)

    def passage_inner_step(block_index, accum):
        first = block_index * passage_block_rows
        sub_block = lax.dynamic_slice_in_dim(passage_segment, first, passage_block_rows, 0)
        block_lse = lax.dynamic_slice_in_dim(all_lse, first, passage_block_rows, 0)
        block_pos = lax.dynamic_slice_in_dim(all_positive, first, passage_block_rows, 0)
        scores = score_block(sub_block, passages)
        weights = jnp.exp(scores - block_lse[:, None]).astype(jnp.bfloat16)
        accum = accum + lax.dot_general(
            weights, sub_block, (((0,), (0,)), ((), ())), preferred_element_type=jnp.float32
        )
        hit_row = block_pos - own_base
        inside = (hit_row >= 0) & (hit_row < per_dev)
        target_slot = jnp.where(inside, hit_row, per_dev).astype(jnp.int32)
        return accum.at[target_slot].add(-sub_block.astype(jnp.float32), mode="drop")

    grad_passages = lax.fori_loop(
        0, length // passage_block_rows, passage_inner_step, passage_start
    )
    grad_queries = lax.psum(query_part, "grp")
    return (losses, grad_queries, grad_passages)


def solution(mesh):
    placed = (P("rows", None), P(("rows", "grp"), None), P("rows"))
    return jax.shard_map(
        local,
        mesh=mesh,
        in_specs=placed,
        out_specs=(P("rows"), P("rows", None), P(("rows", "grp"), None)),
        check_vma=False,
    )
```

profile of v0, /device:TPU:0, one launch (start us, length us, event | category | flops | bytes accessed | tf_op | source)
XLA Modules:
  0.0 205.9 jit_solution(9051152842983273192)
XLA Ops:
  7.2 0.0 all-gather.11.cloned.1.call-start
  7.2 0.7 all-gather.11.cloned.1.call-update
  7.9 0.0 all-gather.13.cloned.1.call-start
  7.9 0.7 all-gather.13.cloned.1.call-update
  8.6 0.0 all-reduce.2.cloned.1.call-start
  8.7 22.8 %all-gather.7 = s32[8,1,256]{2,1,0:T(1,128)S(1)} all-gather(s32[1,1,256]{2,1,0:T(1,128)} %bitcast.77), channel_id=1, replica_groups=mesh['rows'=8,'grp'=4] {'rows'}, dimensions={0}, use_global_device_ids=true | all-gather | bytes 9216 | tf_op jit(solution)/shard_map/all_gather | solution.py:80
  31.6 0.7 compare_select_fusion.3
  32.3 53.4 %all-gather.11.cloned.1.call-done = bf16[2048,1024]{1,0:T(8,128)(2,1)} async-done(((bf16[256,1024]{1,0:T(8,128)(2,1)}), bf16[2048,1024]{1,0:T(8,128)(2,1)}) %all-gather.11.cloned.1.call-update) | async-done | bytes 4194320 | tf_op jit(solution)/shard_map/all_gather | solution.py:55
  85.7 5.5 %while.66 = (s32[]{:T(128)}, f32[256]{0:T(256)S(1)}, f32[256]{0:T(256)S(1)}, f32[256]{0:T(256)S(1)}, bf16[2048,1024]{1,0:T(8,128)(2,1)}, /*index=5*/bf16[256,102...) while((s32[]{:T(128)}, f32[256]{0:T(256)S(1)}, ...), condition=%wide.region_4.5_spmd.clone, body=%wide.region_0.4_spmd.clone.sunk | while | flops 538446336 | bytes 4745398 | solution.py:74
  85.7 2.4 %fusion.64 = (f32[256]{0:T(256)S(1)}, f32[1024,256]{1,0:T(8,128)S(1)}) fusion(bf16[256,1024]{1,0:T(8,128)(2,1)} %get-tuple-element.881, bf16[2048,1024]{1,0:T(8,128)(2,1)} %get-tuple-element.880, s32[]{:T(128)S(6)} %select_n.172), kind=kOutput, calls=%fused_computation.66.clone.1 | convolution fusion | flops 537132800 | bytes 3671044 | tf_op jit(solution)/shard_map/while/body/eval_jaxpr/dot_general | solution.py:21
  88.1 0.3 fusion.66
  88.4 2.4 %fusion.64 = (f32[256]{0:T(256)S(1)}, f32[1024,256]{1,0:T(8,128)S(1)}) fusion(bf16[256,1024]{1,0:T(8,128)(2,1)} %get-tuple-element.881, bf16[2048,1024]{1,0:T(8,128)(2,1)} %get-tuple-element.880, s32[]{:T(128)S(6)} %select_n.172), kind=kOutput, calls=%fused_computation.66.clone.1 | convolution fusion | flops 537132800 | bytes 3671044 | tf_op jit(solution)/shard_map/while/body/eval_jaxpr/dot_general | solution.py:21
  90.9 0.3 fusion.66
  91.2 5.1 %all-gather.3 = f32[4,1,256]{2,1,0:T(1,128)S(1)} all-gather(f32[1,1,256]{2,1,0:T(1,128)S(1)} %bitcast.60), channel_id=2, replica_groups=mesh['rows'=8,'grp'=4] {'grp'}, dimensions={0}, use_global_device_ids=true | all-gather | bytes 5120 | tf_op jit(solution)/shard_map/all_gather | solution.py:11
  96.3 5.1 %all-gather.4 = f32[4,1,256]{2,1,0:T(1,128)S(1)} all-gather(f32[1,1,256]{2,1,0:T(1,128)S(1)} %bitcast.71), channel_id=3, replica_groups=mesh['rows'=8,'grp'=4] {'grp'}, dimensions={0}, use_global_device_ids=true | all-gather | bytes 5120 | tf_op jit(solution)/shard_map/all_gather | solution.py:11
  101.3 5.1 %all-gather.5 = f32[4,1,256]{2,1,0:T(1,128)S(1)} all-gather(f32[1,1,256]{2,1,0:T(1,128)S(1)} %bitcast.72), channel_id=4, replica_groups=mesh['rows'=8,'grp'=4] {'grp'}, dimensions={0}, use_global_device_ids=true | all-gather | bytes 5120 | tf_op jit(solution)/shard_map/all_gather | solution.py:11
  106.4 0.2 while.64
  106.6 0.6 fusion.38
  107.2 18.4 %all-gather.6 = f32[8,1,256]{2,1,0:T(1,128)S(1)} all-gather(f32[1,1,256]{2,1,0:T(1,128)S(1)} %bitcast.76), channel_id=1, replica_groups=mesh['rows'=8,'grp'=4] {'rows'}, dimensions={0}, use_global_device_ids=true | all-gather | bytes 9216 | tf_op jit(solution)/shard_map/all_gather | solution.py:79
  125.6 13.9 %while.67 = (s32[]{:T(128)}, f32[256,1024]{1,0:T(8,128)}, bf16[2048,1024]{1,0:T(8,128)(2,1)}, bf16[256,1024]{1,0:T(8,128)(2,1)}, f32[256]{0:T(256)S(1)}, /*index...) while((s32[]{:T(128)}, f32[256,1024]{1,0:T(8,128)}, ...), condition=%wide.region_8.9_spmd.clone, body=%wide.region_7.8_spmd.clone.sunk | while | flops 1075843584 | bytes 12595401 | solution.py:102
  125.6 0.0 copy-start.1
  125.6 1.8 constant_dynamic-slice_fusion.9
  127.5 1.2 gather_fusion
  128.6 0.0 copy-done.1
  128.7 3.3 %fusion.70 = f32[256,1024]{1,0:T(8,128)} fusion(bf16[1024,1024]{1,0:T(8,128)(2,1)S(1)} %constant_dynamic-slice_fusion.9, f32[256,1024]{1,0:T(8,128)} %get-tuple-element.928, bf16[256,1024]{1,0:T(8,128)(2,1)S(1)} %copy-done.1, bf16[256,1024]{1,0:T(8,128)(2,1)S(1)} %gather_fusion, f32[256]{0:T(256)S(1)} %get-tuple-element.941, ...), kind=kOutput, calls=%fused_computation.37.clone.1 | convolution fusion | flops 1075838976 | bytes 5244417 | tf_op jit(solution)/shard_map/while/body/eval_jaxpr/dot_general | solution.py:94
  131.9 0.0 copy-start.1
  132.0 1.8 constant_dynamic-slice_fusion.9
  133.8 1.2 gather_fusion
  135.0 0.0 copy-done.1
  135.0 4.5 %fusion.70 = f32[256,1024]{1,0:T(8,128)} fusion(bf16[1024,1024]{1,0:T(8,128)(2,1)S(1)} %constant_dynamic-slice_fusion.9, f32[256,1024]{1,0:T(8,128)} %get-tuple-element.928, bf16[256,1024]{1,0:T(8,128)(2,1)S(1)} %copy-done.1, bf16[256,1024]{1,0:T(8,128)(2,1)S(1)} %gather_fusion, f32[256]{0:T(256)S(1)} %get-tuple-element.941, ...), kind=kOutput, calls=%fused_computation.37.clone.1 | convolution fusion | flops 1075838976 | bytes 5244417 | tf_op jit(solution)/shard_map/while/body/eval_jaxpr/dot_general | solution.py:94
  139.5 0.0 all-reduce.2.cloned.1.call-update
  139.5 19.6 %all-gather.13.cloned.1.call-done = bf16[2048,1024]{1,0:T(8,128)(2,1)} async-done(((bf16[256,1024]{1,0:T(8,128)(2,1)}), bf16[2048,1024]{1,0:T(8,128)(2,1)}) %all-gather.13.cloned.1.call-update) | async-done | bytes 4194320 | tf_op jit(solution)/shard_map/all_gather | solution.py:103
  159.2 0.1 broadcast.167
  159.3 29.8 %while.65 = (s32[]{:T(128)}, f32[256,1024]{1,0:T(8,128)S(1)}, bf16[2048,1024]{1,0:T(8,128)(2,1)}, bf16[256,1024]{1,0:T(8,128)(2,1)}, f32[2048]{0:T(1024)S(1)}, /...) while((s32[]{:T(128)}, f32[256,1024]{1,0:T(8,128)S(1)}, ...), condition=%wide.region_12.13_spmd, body=%wide.region_10.12_spmd.sunk | while | flops 1077682176 | bytes 9983667 | solution.py:122
  159.3 4.7 %fusion.62 = f32[256,1024]{1,0:T(8,128)S(1)} fusion(f32[256,1024]{1,0:T(8,128)S(1)} %get-tuple-element.959, bf16[2048,1024]{1,0:T(8,128)(2,1)} %get-tuple-element.971, s32[]{:T(128)S(6)} %select_n.170, bf16[256,1024]{1,0:T(8,128)(2,1)} %get-tuple-element.972, f32[1024]{0:T(1024)S(1)} %dynamic_slice.111), kind=kOutput, calls=%fused_computation.16.clone.1 | convolution fusion | flops 1074528256 | bytes 6820864 | tf_op jit(solution)/shard_map/while/body/eval_jaxpr/dot_general | solution.py:114
  164.1 10.1 %scatter_custom_fusion.5 = f32[256,1024]{1,0:T(8,128)S(1)} fusion(f32[256,1024]{1,0:T(8,128)S(1)} %fusion.62, s32[1024]{0:T(1024)S(1)} %compare_select_fusion.6, bf16[2048,1024]{1,0:T(8,128)(2,1)} %get-tuple-element.971, s32[]{:T(128)S(6)} %select_n.170, s32[]{:T(128)} %constant.224.clone.1..sunk.1), kind=kCustom, calls=%fused_computation.6.clone.1 | custom fusion | flops 3145728 | bytes 3146244 | tf_op jit(solution)/shard_map/while/body/eval_jaxpr/scatter-add | solution.py:120
  174.2 4.7 %fusion.62 = f32[256,1024]{1,0:T(8,128)S(1)} fusion(f32[256,1024]{1,0:T(8,128)S(1)} %get-tuple-element.959, bf16[2048,1024]{1,0:T(8,128)(2,1)} %get-tuple-element.971, s32[]{:T(128)S(6)} %select_n.170, bf16[256,1024]{1,0:T(8,128)(2,1)} %get-tuple-element.972, f32[1024]{0:T(1024)S(1)} %dynamic_slice.111), kind=kOutput, calls=%fused_computation.16.clone.1 | convolution fusion | flops 1074528256 | bytes 6820864 | tf_op jit(solution)/shard_map/while/body/eval_jaxpr/dot_general | solution.py:114
  179.0 10.1 %scatter_custom_fusion.5 = f32[256,1024]{1,0:T(8,128)S(1)} fusion(f32[256,1024]{1,0:T(8,128)S(1)} %fusion.62, s32[1024]{0:T(1024)S(1)} %compare_select_fusion.6, bf16[2048,1024]{1,0:T(8,128)(2,1)} %get-tuple-element.971, s32[]{:T(128)S(6)} %select_n.170, s32[]{:T(128)} %constant.224.clone.1..sunk.1), kind=kCustom, calls=%fused_computation.6.clone.1 | custom fusion | flops 3145728 | bytes 3146244 | tf_op jit(solution)/shard_map/while/body/eval_jaxpr/scatter-add | solution.py:120
  189.1 0.0 copy-start
  189.1 7.9 %all-reduce.2.cloned.1.call-done = f32[256,1024]{1,0:T(8,128)} async-done(((f32[256,1024]{1,0:T(8,128)}), f32[256,1024]{1,0:T(8,128)}) %all-reduce.2.cloned.1.call-update) | async-done | bytes 1048592 | tf_op jit(solution)/shard_map/psum | solution.py:125
  197.0 2.3 %copy.53 = f32[256,1024]{1,0:T(8,128)} copy(f32[256,1024]{1,0:T(8,128)} %all-reduce.2.cloned.1.call-done) | data formatting | bytes 2097152
  199.3 0.0 copy-done
  (40 shorter events, 0.3 us)
Async XLA Ops:
  7.2 78.5 %all-gather.11.cloned.1.call-start = ((), (), s32[]{:S(2)}) async-start(), calls=%async_computation | async-start | bytes 4718592 | tf_op jit(solution)/shard_map/all_gather | solution.py:55
  7.9 151.3 %all-gather.13.cloned.1.call-start = ((), (), s32[]{:S(2)}) async-start(), calls=%async_computation.2 | async-start | bytes 4718592 | tf_op jit(solution)/shard_map/all_gather | solution.py:103
  8.6 188.4 %all-reduce.2.cloned.1.call-start = ((), (), s32[]{:S(2)}) async-start(), calls=%async_computation.1 | async-start | bytes 2097152 | tf_op jit(solution)/shard_map/psum | solution.py:125
  125.6 3.1 %copy-start.1 = (bf16[256,1024]{1,0:T(8,128)(2,1)S(1)}, bf16[256,1024]{1,0:T(8,128)(2,1)}, u32[]{:S(2)}) copy-start(bf16[256,1024]{1,0:T(8,128)(2,1)} %get-tuple-element.940) | copy-start | bytes 1572868 | tf_op jit(solution)/shard_map/while
  131.9 3.0 %copy-start.1 = (bf16[256,1024]{1,0:T(8,128)(2,1)S(1)}, bf16[256,1024]{1,0:T(8,128)(2,1)}, u32[]{:S(2)}) copy-start(bf16[256,1024]{1,0:T(8,128)(2,1)} %get-tuple-element.940) | copy-start | bytes 1572868 | tf_op jit(solution)/shard_map/while
  189.1 10.2 %copy-start = (f32[256,1024]{1,0:T(8,128)}, f32[256,1024]{1,0:T(8,128)S(1)}, u32[]{:S(2)}) copy-start(f32[256,1024]{1,0:T(8,128)S(1)} %get-tuple-element.982) | copy-start | bytes 3145732
Sparse Core Ops, SparseCore 0:
  10.1 75.5 all-gather.10
  87.8 71.3 all-gather.12
  162.1 34.8 all-reduce.1
where the time goes:
time: 206 us
  waiting for transfers between devices  82.3 us (40%)
  blocking collectives  56.4 us (27%)
  other arithmetic  22.2 us (11%)
  matrix products  22.1 us (11%)
  between operations  13.8 us (7%)
  local copies, waits for them, and re-layouts  8.5 us (4%)
    all_gather x1, waiting for transfers between devices, local(): segment = lax.all_gather(passages, 'rows', axis=0, tiled=True)  53.4 us
    all_gather x1, blocking collectives, local(): lax.all_gather(positive, 'rows', axis=0, tiled=True)  22.8 us
    scatter-add x2, other arithmetic, passage_inner_step(): accum.at[target_slot].add(-sub_block.astype(jnp.float32), mode='drop')  20.2 us
    all_gather x1, waiting for transfers between devices, local(): passage_segment = lax.all_gather(queries, 'rows', axis=0, tiled=True)  19.6 us
    all_gather x1, blocking collectives, local(): lax.all_gather(log_total, 'rows', axis=0, tiled=True)  18.4 us
    all_gather x3, blocking collectives, combined_all(): everything = jax.tree.map(lambda part: lax.all_gather(part, axis), value)  15.2 us
    dot_general x2, matrix products, passage_inner_step(): lax.dot_general(weights, sub_block, (((0,), (0,)), ((), ())), preferred_e...  9.45 us
    psum x1, waiting for transfers between devices, local(): grad_queries = lax.psum(query_part, 'grp')  7.93 us
  transfers between devices with their start and end apart: 3, of which 3 were waited for; matrix products, arithmetic and copies ran while one was open for 25% of the time, Pallas kernels for 0%

commit v1 on v0

--- a/solution.py
+++ b/solution.py
@@ -52,7 +52,12 @@
         jnp.zeros((rows_q,), jnp.float32),
         jnp.zeros((rows_q,), jnp.float32),
     )
-    segment = lax.all_gather(passages, "rows", axis=0, tiled=True)
+    ring = [passages]
+    for hop in range(7):
+        ring.append(lax.ppermute(ring[-1], "rows", [(dev, (dev + 1) % 8) for dev in range(8)]))
+    segment = jnp.roll(
+        jnp.concatenate(ring[::-1], axis=0), (lax.axis_index("rows") + 1) * ring[0].shape[0], axis=0
+    )
     length = segment.shape[0]
     block_rows = block_size(length)
 

time: 206 us -> 268 us (1.30)
  waiting for transfers between devices: 82.3 us -> 131 us
  local copies, waits for them, and re-layouts: 8.5 us -> 15.5 us
  starting transfers between devices: 0.11 us -> 3.46 us
    ppermute x0 -> x7, waiting for transfers between devices: none -> 128 us  [local(): lax.ppermute(ring[-1], 'rows', [(dev, (dev + 1) % 8) for dev in range(8)])]
    all_gather x1, waiting for transfers between devices: 53.4 us -> 0.01 us  [local(): query_segment = lax.all_gather(passages, 'rows', axis=0, tiled=True)]
    all_gather x1, waiting for transfers between devices: 19.6 us -> 0.02 us  [local(): passage_segment = lax.all_gather(queries, 'rows', axis=0, tiled=True)]
    psum x1, waiting for transfers between devices: 7.93 us -> 2.61 us  [local(): grad_queries = lax.psum(query_part, 'grp')]
    unnamed x6 -> x23, local copies, waits for them, and re-layouts: 2.32 us -> 7.03 us
    ppermute x0 -> x7, starting transfers between devices: none -> 3.34 us  [local(): lax.ppermute(ring[-1], 'rows', [(dev, (dev + 1) % 8) for dev in range(8)])]
  transfers between devices with their start and end apart: 3 -> 10, of which waited for: 3 -> 7; matrix products, arithmetic and copies ran while one was open for 25% -> 22% of each run, Pallas kernels for 0% -> 0%
where the time goes in v1:
time: 268 us; the launch traced here: 267 us
  waiting for transfers between devices  131 us (49%)
  blocking collectives  56.8 us (21%)
  matrix products  23.4 us (9%)
  other arithmetic  22.2 us (8%)
  local copies, waits for them, and re-layouts  15.5 us (6%)
  between operations  14 us (5%)
  starting transfers between devices  3.46 us (1%)
    ppermute x7, waiting for transfers between devices, local(): lax.ppermute(ring[-1], 'rows', [(dev, (dev + 1) % 8) for dev in range(8)])  128 us
    all_gather x1, blocking collectives, local(): lax.all_gather(positive, 'rows', axis=0, tiled=True)  22.4 us
    scatter-add x2, other arithmetic, passage_inner_step(): accum.at[target_slot].add(-sub_block.astype(jnp.float32), mode='drop')  20.2 us
    all_gather x1, blocking collectives, local(): lax.all_gather(log_total, 'rows', axis=0, tiled=True)  19.2 us
    all_gather x3, blocking collectives, combined_all(): everything = jax.tree.map(lambda part: lax.all_gather(part, axis), value)  15.2 us
    dot_general x2, matrix products, passage_inner_step(): lax.dot_general(weights, sub_block, (((0,), (0,)), ((), ())), preferred_e...  9.28 us
    dot_general x2, matrix products, query_inner_step(): jnp.dot(weights, sub_block, preferred_element_type=jnp.float32)  9 us
    unnamed x23, local copies, waits for them, and re-layouts  7.03 us
  transfers between devices with their start and end apart: 10, of which 7 were waited for; matrix products, arithmetic and copies ran while one was open for 22% of the time, Pallas kernels for 0%

profile of v1, /device:TPU:0, one launch (start us, length us, event | category | flops | bytes accessed | tf_op | source)
XLA Modules:
  0.0 267.0 jit_solution(2970793329674586530)
XLA Ops:
  7.2 0.0 copy-start
  7.2 0.0 all-gather.11.cloned.1.call-start
  7.2 0.7 all-gather.11.cloned.1.call-update
  7.9 0.0 all-gather.13.cloned.1.call-start
  8.0 3.0 %collective-permute-start = (bf16[256,1024]{1,0:T(8,128)(2,1)}, bf16[256,1024]{1,0:T(8,128)(2,1)S(1)}, u32[]{:S(2)}, u32[]{:S(2)}) collective-permute-start(bf16[256,1024]{1,0:T(8,128)(2,1)} %param.12), channel_id=1, source_target_pairs={{0,4},{4,8},{8,12},{12,16},{16,20},{20,24},{24,28},{28,0},{1,5},{5... | collective-permute-start | bytes 1572872 | tf_op jit(solution)/shard_map/ppermute | solution.py:57
  11.0 15.3 %collective-permute-done = bf16[256,1024]{1,0:T(8,128)(2,1)S(1)} collective-permute-done((bf16[256,1024]{1,0:T(8,128)(2,1)}, bf16[256,1024]{1,0:T(8,128)(2,1)S(1)}, u32[]{:S(2)}, u32[]{:S(2)}) %collective-permute-start) | collective-permute-done | bytes 524320 | tf_op jit(solution)/shard_map/ppermute | solution.py:57
  26.3 0.3 collective-permute-start.1
  26.6 27.8 %collective-permute-done.1 = bf16[256,1024]{1,0:T(8,128)(2,1)S(1)} collective-permute-done((bf16[256,1024]{1,0:T(8,128)(2,1)S(1)}, bf16[256,1024]{1,0:T(8,128)(2,1)S(1)}, u32[]{:S(2)}, u32[]{:S(2)}) %collective-permute-start.1) | collective-permute-done | bytes 524320 | tf_op jit(solution)/shard_map/ppermute | solution.py:57
  54.4 0.0 collective-permute-start.2
  54.4 25.2 %collective-permute-done.2 = bf16[256,1024]{1,0:T(8,128)(2,1)S(1)} collective-permute-done((bf16[256,1024]{1,0:T(8,128)(2,1)S(1)}, bf16[256,1024]{1,0:T(8,128)(2,1)S(1)}, u32[]{:S(2)}, u32[]{:S(2)}) %collective-permute-start.2) | collective-permute-done | bytes 524320 | tf_op jit(solution)/shard_map/ppermute | solution.py:57
  79.6 0.0 collective-permute-start.3
  79.6 26.9 %collective-permute-done.3 = bf16[256,1024]{1,0:T(8,128)(2,1)S(1)} collective-permute-done((bf16[256,1024]{1,0:T(8,128)(2,1)S(1)}, bf16[256,1024]{1,0:T(8,128)(2,1)S(1)}, u32[]{:S(2)}, u32[]{:S(2)}) %collective-permute-start.3) | collective-permute-done | bytes 524320 | tf_op jit(solution)/shard_map/ppermute | solution.py:57
  106.5 0.0 collective-permute-start.4
  106.5 19.1 %collective-permute-done.4 = bf16[256,1024]{1,0:T(8,128)(2,1)S(1)} collective-permute-done((bf16[256,1024]{1,0:T(8,128)(2,1)S(1)}, bf16[256,1024]{1,0:T(8,128)(2,1)S(1)}, u32[]{:S(2)}, u32[]{:S(2)}) %collective-permute-start.4) | collective-permute-done | bytes 524320 | tf_op jit(solution)/shard_map/ppermute | solution.py:57
  125.6 0.0 collective-permute-start.5
  125.6 13.6 %collective-permute-done.5 = bf16[256,1024]{1,0:T(8,128)(2,1)} collective-permute-done((bf16[256,1024]{1,0:T(8,128)(2,1)S(1)}, bf16[256,1024]{1,0:T(8,128)(2,1)}, u32[]{:S(2)}, u32[]{:S(2)}) %collective-permute-start.5) | collective-permute-done | bytes 524320 | tf_op jit(solution)/shard_map/ppermute | solution.py:57
  139.3 0.0 collective-permute-start.6
  139.3 0.0 all-gather.13.cloned.1.call-update
  139.3 0.0 all-reduce.2.cloned.1.call-start
  139.4 22.4 %all-gather.7 = s32[8,1,256]{2,1,0:T(1,128)S(1)} all-gather(s32[1,1,256]{2,1,0:T(1,128)} %bitcast.77), channel_id=1, replica_groups=mesh['rows'=8,'grp'=4] {'rows'}, dimensions={0}, use_global_device_ids=true | all-gather | bytes 9216 | tf_op jit(solution)/shard_map/all_gather | solution.py:85
  161.8 0.7 compare_select_fusion.3
  162.5 0.0 collective-permute-done.6
  162.5 1.1 constant_dynamic-update-slice_fusion.15
  163.6 1.1 constant_dynamic-update-slice_fusion.14
  164.9 0.0 copy-done
  164.9 1.1 constant_dynamic-update-slice_fusion.7
  166.0 1.1 constant_dynamic-update-slice_fusion.6
  167.3 2.4 constant_dynamic-slice_fusion.4
  169.8 5.8 %while.66 = (s32[]{:T(128)}, f32[256]{0:T(256)S(1)}, f32[256]{0:T(256)S(1)}, f32[256]{0:T(256)S(1)}, bf16[2048,1024]{1,0:T(8,128)(2,1)}, /*index=5*/bf16[256,102...) while((s32[]{:T(128)}, f32[256]{0:T(256)S(1)}, ...), condition=%wide.region_4.5_spmd.clone, body=%wide.region_0.4_spmd.clone.sunk | while | flops 538446336 | bytes 4745390 | solution.py:79
  169.8 2.4 fusion.64
  172.2 0.3 fusion.66
  172.5 2.7 fusion.64
  175.2 0.3 fusion.66
  175.5 5.1 %all-gather.3 = f32[4,1,256]{2,1,0:T(1,128)S(1)} all-gather(f32[1,1,256]{2,1,0:T(1,128)S(1)} %bitcast.60), channel_id=2, replica_groups=mesh['rows'=8,'grp'=4] {'grp'}, dimensions={0}, use_global_device_ids=true | all-gather | bytes 5120 | tf_op jit(solution)/shard_map/all_gather | solution.py:11
  180.6 5.1 %all-gather.4 = f32[4,1,256]{2,1,0:T(1,128)S(1)} all-gather(f32[1,1,256]{2,1,0:T(1,128)S(1)} %bitcast.71), channel_id=3, replica_groups=mesh['rows'=8,'grp'=4] {'grp'}, dimensions={0}, use_global_device_ids=true | all-gather | bytes 5120 | tf_op jit(solution)/shard_map/all_gather | solution.py:11
  185.7 5.1 %all-gather.5 = f32[4,1,256]{2,1,0:T(1,128)S(1)} all-gather(f32[1,1,256]{2,1,0:T(1,128)S(1)} %bitcast.72), channel_id=4, replica_groups=mesh['rows'=8,'grp'=4] {'grp'}, dimensions={0}, use_global_device_ids=true | all-gather | bytes 5120 | tf_op jit(solution)/shard_map/all_gather | solution.py:11
  190.7 0.2 while.64
  191.0 0.6 fusion.38
  191.5 19.2 %all-gather.6 = f32[8,1,256]{2,1,0:T(1,128)S(1)} all-gather(f32[1,1,256]{2,1,0:T(1,128)S(1)} %bitcast.76), channel_id=1, replica_groups=mesh['rows'=8,'grp'=4] {'rows'}, dimensions={0}, use_global_device_ids=true | all-gather | bytes 9216 | tf_op jit(solution)/shard_map/all_gather | solution.py:84
  210.8 0.0 all-gather.11.cloned.1.call-done
  210.8 15.0 %while.67 = (s32[]{:T(128)}, f32[256,1024]{1,0:T(8,128)}, bf16[2048,1024]{1,0:T(8,128)(2,1)}, bf16[256,1024]{1,0:T(8,128)(2,1)}, f32[256]{0:T(256)S(1)}, /*index...) while((s32[]{:T(128)}, f32[256,1024]{1,0:T(8,128)}, ...), condition=%wide.region_8.9_spmd.clone, body=%wide.region_7.8_spmd.clone.sunk | while | flops 1075843584 | bytes 10498213 | solution.py:107
  210.8 1.8 constant_dynamic-slice_fusion.10
  212.6 1.2 gather_fusion
  213.8 4.3 %fusion.70 = f32[256,1024]{1,0:T(8,128)} fusion(bf16[1024,1024]{1,0:T(8,128)(2,1)S(1)} %constant_dynamic-slice_fusion.10, f32[256,1024]{1,0:T(8,128)} %get-tuple-element.928, bf16[256,1024]{1,0:T(8,128)(2,1)} %get-tuple-element.940, bf16[256,1024]{1,0:T(8,128)(2,1)S(1)} %gather_fusion, f32[256]{0:T(256)S(1)} %get-tuple-element.941, ...), kind=kOutput, calls=%fused_computation.37.clone.1 | convolution fusion | flops 1075838976 | bytes 5244417 | tf_op jit(solution)/shard_map/while/body/eval_jaxpr/dot_general | solution.py:99
  218.1 1.8 constant_dynamic-slice_fusion.10
  219.9 1.2 gather_fusion
  221.1 4.7 %fusion.70 = f32[256,1024]{1,0:T(8,128)} fusion(bf16[1024,1024]{1,0:T(8,128)(2,1)S(1)} %constant_dynamic-slice_fusion.10, f32[256,1024]{1,0:T(8,128)} %get-tuple-element.928, bf16[256,1024]{1,0:T(8,128)(2,1)} %get-tuple-element.940, bf16[256,1024]{1,0:T(8,128)(2,1)S(1)} %gather_fusion, f32[256]{0:T(256)S(1)} %get-tuple-element.941, ...), kind=kOutput, calls=%fused_computation.37.clone.1 | convolution fusion | flops 1075838976 | bytes 5244417 | tf_op jit(solution)/shard_map/while/body/eval_jaxpr/dot_general | solution.py:99
  225.7 0.0 all-reduce.2.cloned.1.call-update
  225.8 0.0 all-gather.13.cloned.1.call-done
  225.8 0.1 broadcast.168
  225.9 29.6 %while.65 = (s32[]{:T(128)}, f32[256,1024]{1,0:T(8,128)S(1)}, bf16[2048,1024]{1,0:T(8,128)(2,1)}, bf16[256,1024]{1,0:T(8,128)(2,1)S(1)}, f32[2048]{0:T(1024)S(1)...) while((s32[]{:T(128)}, f32[256,1024]{1,0:T(8,128)S(1)}, ...), condition=%wide.region_12.13_spmd, body=%wide.region_10.12_spmd.sunk | while | flops 1077682176 | bytes 9983659 | solution.py:127
  225.9 4.7 %fusion.62 = f32[256,1024]{1,0:T(8,128)S(1)} fusion(f32[256,1024]{1,0:T(8,128)S(1)} %get-tuple-element.959, bf16[2048,1024]{1,0:T(8,128)(2,1)} %get-tuple-element.971, s32[]{:T(128)S(6)} %select_n.184, bf16[256,1024]{1,0:T(8,128)(2,1)S(1)} %get-tuple-element.972, f32[1024]{0:T(1024)S(1)} %dynamic_slice.117), kind=kOutput, calls=%fused_computation.16.clone.1 | convolution fusion | flops 1074528256 | bytes 6820864 | tf_op jit(solution)/shard_map/while/body/eval_jaxpr/dot_general | solution.py:119
  230.7 10.1 %scatter_custom_fusion.5 = f32[256,1024]{1,0:T(8,128)S(1)} fusion(f32[256,1024]{1,0:T(8,128)S(1)} %fusion.62, s32[1024]{0:T(1024)S(1)} %compare_select_fusion.6, bf16[2048,1024]{1,0:T(8,128)(2,1)} %get-tuple-element.971, s32[]{:T(128)S(6)} %select_n.184, s32[]{:T(128)} %constant.242.clone.1..sunk.1), kind=kCustom, calls=%fused_computation.6.clone.1 | custom fusion | flops 3145728 | bytes 3146244 | tf_op jit(solution)/shard_map/while/body/eval_jaxpr/scatter-add | solution.py:125
  240.9 4.5 %fusion.62 = f32[256,1024]{1,0:T(8,128)S(1)} fusion(f32[256,1024]{1,0:T(8,128)S(1)} %get-tuple-element.959, bf16[2048,1024]{1,0:T(8,128)(2,1)} %get-tuple-element.971, s32[]{:T(128)S(6)} %select_n.184, bf16[256,1024]{1,0:T(8,128)(2,1)S(1)} %get-tuple-element.972, f32[1024]{0:T(1024)S(1)} %dynamic_slice.117), kind=kOutput, calls=%fused_computation.16.clone.1 | convolution fusion | flops 1074528256 | bytes 6820864 | tf_op jit(solution)/shard_map/while/body/eval_jaxpr/dot_general | solution.py:119
  245.4 10.1 %scatter_custom_fusion.5 = f32[256,1024]{1,0:T(8,128)S(1)} fusion(f32[256,1024]{1,0:T(8,128)S(1)} %fusion.62, s32[1024]{0:T(1024)S(1)} %compare_select_fusion.6, bf16[2048,1024]{1,0:T(8,128)(2,1)} %get-tuple-element.971, s32[]{:T(128)S(6)} %select_n.184, s32[]{:T(128)} %constant.242.clone.1..sunk.1), kind=kCustom, calls=%fused_computation.6.clone.1 | custom fusion | flops 3145728 | bytes 3146244 | tf_op jit(solution)/shard_map/while/body/eval_jaxpr/scatter-add | solution.py:125
  255.6 0.0 copy-start.1
  255.6 2.6 all-reduce.2.cloned.1.call-done
  258.2 2.3 copy.68
  260.5 0.0 copy-done.1
  (52 shorter events, 0.8 us)
Async XLA Ops:
  7.2 157.7 %copy-start = (bf16[256,1024]{1,0:T(8,128)(2,1)S(1)}, bf16[256,1024]{1,0:T(8,128)(2,1)}, u32[]{:S(2)}) copy-start(bf16[256,1024]{1,0:T(8,128)(2,1)} %param.12) | copy-start | bytes 1572868
  7.2 203.6 %all-gather.11.cloned.1.call-start = ((), (), s32[]{:S(2)}) async-start(), calls=%async_computation | async-start | bytes 4718592 | tf_op jit(solution)/shard_map/all_gather | solution.py:90
  7.9 217.9 %all-gather.13.cloned.1.call-start = ((), (), s32[]{:S(2)}) async-start(), calls=%async_computation.2 | async-start | bytes 4718592 | tf_op jit(solution)/shard_map/all_gather | solution.py:108
  8.0 18.3 %collective-permute-start = (bf16[256,1024]{1,0:T(8,128)(2,1)}, bf16[256,1024]{1,0:T(8,128)(2,1)S(1)}, u32[]{:S(2)}, u32[]{:S(2)}) collective-permute-start(bf16[256,1024]{1,0:T(8,128)(2,1)} %param.12), channel_id=1, source_target_pairs={{0,4},{4,8},{8,12},{12,16},{16,20},{20,24},{24,28},{28,0},{1,5},{5... | collective-permute-start | bytes 1572872 | tf_op jit(solution)/shard_map/ppermute | solution.py:57
  26.3 28.1 %collective-permute-start.1 = (bf16[256,1024]{1,0:T(8,128)(2,1)S(1)}, bf16[256,1024]{1,0:T(8,128)(2,1)S(1)}, u32[]{:S(2)}, u32[]{:S(2)}) collective-permute-start(bf16[256,1024]{1,0:T(8,128)(2,1)S(1)} %collective-permute-done), channel_id=1, source_target_pairs={{0,4},{4,8},{8,12},{12,16},{16,20},{20,24},{24,28},{28,0},{1,5},{5... | collective-permute-start | bytes 1572872 | tf_op jit(solution)/shard_map/ppermute | solution.py:57
  54.4 25.2 %collective-permute-start.2 = (bf16[256,1024]{1,0:T(8,128)(2,1)S(1)}, bf16[256,1024]{1,0:T(8,128)(2,1)S(1)}, u32[]{:S(2)}, u32[]{:S(2)}) collective-permute-start(bf16[256,1024]{1,0:T(8,128)(2,1)S(1)} %collective-permute-done.1), channel_id=1, source_target_pairs={{0,4},{4,8},{8,12},{12,16},{16,20},{20,24},{24,28},{28,0},{1,5},{5... | collective-permute-start | bytes 1572872 | tf_op jit(solution)/shard_map/ppermute | solution.py:57
  79.6 26.9 %collective-permute-start.3 = (bf16[256,1024]{1,0:T(8,128)(2,1)S(1)}, bf16[256,1024]{1,0:T(8,128)(2,1)S(1)}, u32[]{:S(2)}, u32[]{:S(2)}) collective-permute-start(bf16[256,1024]{1,0:T(8,128)(2,1)S(1)} %collective-permute-done.2), channel_id=1, source_target_pairs={{0,4},{4,8},{8,12},{12,16},{16,20},{20,24},{24,28},{28,0},{1,5},{5... | collective-permute-start | bytes 1572872 | tf_op jit(solution)/shard_map/ppermute | solution.py:57
  106.5 19.1 %collective-permute-start.4 = (bf16[256,1024]{1,0:T(8,128)(2,1)S(1)}, bf16[256,1024]{1,0:T(8,128)(2,1)S(1)}, u32[]{:S(2)}, u32[]{:S(2)}) collective-permute-start(bf16[256,1024]{1,0:T(8,128)(2,1)S(1)} %collective-permute-done.3), channel_id=1, source_target_pairs={{0,4},{4,8},{8,12},{12,16},{16,20},{20,24},{24,28},{28,0},{1,5},{5... | collective-permute-start | bytes 1572872 | tf_op jit(solution)/shard_map/ppermute | solution.py:57
  125.6 13.6 %collective-permute-start.5 = (bf16[256,1024]{1,0:T(8,128)(2,1)S(1)}, bf16[256,1024]{1,0:T(8,128)(2,1)}, u32[]{:S(2)}, u32[]{:S(2)}) collective-permute-start(bf16[256,1024]{1,0:T(8,128)(2,1)S(1)} %collective-permute-done.4), channel_id=1, source_target_pairs={{0,4},{4,8},{8,12},{12,16},{16,20},{20,24},{24,28},{28,0},{1,5},{5... | collective-permute-start | bytes 1572872 | tf_op jit(solution)/shard_map/ppermute | solution.py:57
  139.3 23.2 %collective-permute-start.6 = (bf16[256,1024]{1,0:T(8,128)(2,1)}, bf16[256,1024]{1,0:T(8,128)(2,1)}, u32[]{:S(2)}, u32[]{:S(2)}) collective-permute-start(bf16[256,1024]{1,0:T(8,128)(2,1)} %collective-permute-done.5), channel_id=1, source_target_pairs={{0,4},{4,8},{8,12},{12,16},{16,20},{20,24},{24,28},{28,0},{1,5},{5... | collective-permute-start | bytes 1572872 | tf_op jit(solution)/shard_map/ppermute | solution.py:57
  139.3 118.9 %all-reduce.2.cloned.1.call-start = ((), (), s32[]{:S(2)}) async-start(), calls=%async_computation.1 | async-start | bytes 2097152 | tf_op jit(solution)/shard_map/psum | solution.py:130
  255.6 4.9 %copy-start.1 = (f32[256,1024]{1,0:T(8,128)}, f32[256,1024]{1,0:T(8,128)S(1)}, u32[]{:S(2)}) copy-start(f32[256,1024]{1,0:T(8,128)S(1)} %get-tuple-element.982) | copy-start | bytes 3145732
Sparse Core Ops, SparseCore 0:
  10.1 103.9 all-gather.10
  139.4 73.6 all-gather.12
  225.9 32.2 all-reduce.1
